TPU v7x, 128 devices: a whole 4x4x4 slice. The times are simulated.
128 devices in a mesh: south: 4 (over x), east: 8 (over y, core), down: 4 (over z).
Axes of the slice: x: 4, y: 4, z: 4, core: 2. Of those that a mesh axis runs over, the one named last changes fastest.
Arguments:
- field_now: float32 [32, 128, 512, 128], P('south', 'east', 'down'), may hold values from 0.2 to 1.8
- earlier: float32 [32, 128, 512, 128], P('south', 'east', 'down'), may hold values from 0.2 to 1.8
- speed_square: float32 [32, 128, 512, 128], P('south', 'east', 'down'), may hold values from 0.05 to 0.3
Outputs:
- running_total: float32 [32, 128, 512, 128], P('south', 'east', 'down')
- field_now_end: float32 [32, 128, 512, 128], P('south', 'east', 'down')
All inputs are finite; a program needn't handle non-finite values.
Results may differ from a plain program's by a relative error of at most 0.00002.
Values sent between devices are 32-bit elements; how exact they have to be, the bound alone decides.
No kernel may reach another device: no remote copies, remote signals or barrier semaphores. Data moves between devices by JAX's collectives and lax.ppermute only.
A program may use at most 320 MiB of HBM per device.

v0:
```python
import jax
import jax.numpy as jnp
from jax import lax
from jax.sharding import PartitionSpec as P

STEPS = 4


def with_halo(array, sides, width):
    edges = {}
    for axis, dim in sides:
        count, length = (lax.axis_size(axis), array.shape[dim])
        up = [(i, (i + 1) % count) for i in range(count - 1)]
        last = lax.slice_in_dim(array, length - width, length, axis=dim)
        initial = lax.slice_in_dim(array, 0, width, axis=dim)
        edges[dim] = (
            lax.ppermute(last, axis, up),
            lax.ppermute(initial, axis, [(b, a) for a, b in up]),
        )
    done = []
    for _, dim in sides:
        low, high = edges[dim]
        around = [(width, width) if d in done else (0, 0) for d in range(array.ndim)]
        array = jnp.concatenate([jnp.pad(low, around), array, jnp.pad(high, around)], axis=dim)
        done.append(dim)
    return array


def prefix(part, axis, combine, identity):
    place = lax.axis_index(axis)
    gathered = lax.all_gather(part, axis)
    state = jnp.zeros_like(part) + jnp.asarray(identity, part.dtype)

    def one(turn, state):
        return combine(state, lax.dynamic_index_in_dim(gathered, turn, 0, False))

    return lax.fori_loop(0, place, one, state)


def strip_edges(values, dims):
    for dim in dims:
        values = lax.slice_in_dim(values, 1, values.shape[dim] - 1, axis=dim)
    return values


def neighbour(values, dim, start, dims):
    others = [other for other in dims if other != dim]
    values = strip_edges(values, others)
    return lax.slice_in_dim(values, start, start + values.shape[dim] - 2, axis=dim)


def one_step(padded, before, speed_square):
    middle = strip_edges(padded, (0, 1, 2))
    lower = [neighbour(padded, dim, 0, (0, 1, 2)) for dim in (0, 1, 2)]
    upper = [neighbour(padded, dim, 2, (0, 1, 2)) for dim in (0, 1, 2)]
    spread = lower[0] + upper[0] + lower[1] + upper[1] + lower[2] + upper[2] - 6.0 * middle
    return 2.0 * middle - before + speed_square * spread


def shards(field_now, earlier, speed_square):
    for step in range(STEPS):
        padded = with_halo(field_now, (("south", 0), ("east", 1), ("down", 2)), 1)
        later = one_step(padded, earlier, speed_square)
        earlier, field_now = (field_now, later)
    here = jnp.cumsum(field_now, axis=0)
    total = lax.slice_in_dim(here, here.shape[0] - 1, here.shape[0], axis=0)

    def add_pair(earlier_total, later_total):
        return earlier_total + later_total

    below = prefix(total, "south", add_pair, jnp.zeros_like(total))
    running_total = (here + below) / (field_now.shape[0] * lax.axis_size("south"))
    return (running_total, field_now)


def solution(mesh):
    placed = (
        P("south", "east", "down", None),
        P("south", "east", "down", None),
        P("south", "east", "down", None),
    )
    return jax.shard_map(
        shards,
        mesh=mesh,
        in_specs=placed,
        out_specs=(P("south", "east", "down", None), P("south", "east", "down", None)),
        check_vma=False,
    )
```

profile of v0, /device:TPU:14, one launch (start us, length us, event | category | flops | bytes accessed | tf_op | source)
XLA Modules:
  0.0 323.2 jit_solution(2014024687277370611)
XLA Ops:
  7.2 1.8 fusion.51
  10.6 4.6 %collective-permute-start.1 = (f32[1,16,128,128]{3,2,1,0:T(8,128)S(1)}, f32[1,16,128,128]{3,2,1,0:T(8,128)S(1)}, u32[]{:S(2)}, u32[]{:S(2)}) collective-permute-start(f32[1,16,128,128]{3,2,1,0:T(8,128)S(1)} %get-tuple-element.64), channel_id=1, source_target_pairs={{32,0},{64,32},{96,64},{33,1},{65,33},{97,65},{34,2},{66,34},{98,6... | collective-permute-start | bytes 3145736 | tf_op jit(solution)/shard_map/ppermute | solution.py:18
  16.5 1.9 collective-permute-start.2
  18.5 3.6 %collective-permute-start.3 = (f32[8,1,128,128]{3,2,1,0:T(8,128)S(1)}, f32[8,1,128,128]{3,2,1,0:T(8,128)S(1)}, u32[]{:S(2)}, u32[]{:S(2)}) collective-permute-start(f32[8,1,128,128]{3,2,1,0:T(8,128)S(1)} %get-tuple-element.63), channel_id=1, source_target_pairs={{4,0},{8,4},{12,8},{16,12},{20,16},{24,20},{28,24},{5,1},{9,5},{13... | collective-permute-start | bytes 1572872 | tf_op jit(solution)/shard_map/ppermute | solution.py:18
  23.4 3.8 %collective-permute-start.4 = (f32[8,16,1,128]{3,2,1,0:T(1,128)S(1)}, f32[8,16,1,128]{3,2,1,0:T(1,128)S(1)}, u32[]{:S(2)}, u32[]{:S(2)}) collective-permute-start(f32[8,16,1,128]{3,2,1,0:T(1,128)S(1)} %get-tuple-element.60), channel_id=1, source_target_pairs={{0,1},{1,2},{2,3},{4,5},{5,6},{6,7},{8,9},{9,10},{10,11},{12,13},{... | collective-permute-start | bytes 196616 | tf_op jit(solution)/shard_map/ppermute | solution.py:17
  30.4 5.8 %collective-permute-done = f32[1,16,128,128]{3,2,1,0:T(8,128)S(1)} collective-permute-done((f32[1,16,128,128]{3,2,1,0:T(8,128)S(1)}, f32[1,16,128,128]{3,2,1,0:T(8,128)S(1)}, u32[]{:S(2)}, u32[]{:S(2)}) %collective-permute-start) | collective-permute-done | bytes 1048608 | tf_op jit(solution)/shard_map/ppermute | solution.py:17
  37.2 4.8 %constant_dynamic-update-slice_fusion.1 = f32[10,16,128,128]{3,2,1,0:T(8,128)} fusion(f32[10,16,128,128]{3,2,1,0:T(8,128)} %constant_dynamic-update-slice_fusion.2, f32[8,16,128,128]{3,2,1,0:T(8,128)S(1)} %copy-done), kind=kLoop, calls=%fused_computation.109 | loop fusion | bytes 16777216
  44.0 28.2 %fusion.34 = f32[8,16,128,128]{3,2,1,0:T(8,128)} fusion(f32[8,16,128,128]{3,2,1,0:T(8,128)S(1)} %bitcast.10, f32[8,16,1,128]{3,2,1,0:T(1,128)S(1)} %collective-permute-done.5, f32[10,1,128,128]{3,2,1,0:T(8,128)} %pad.51, f32[10,16,128,128]{3,2,1,0:T(8,128)} %constant_dynamic-update-slice_fusion, f32[10,1,128,128]{3,2,1,0:T(8,128)} %pad.50, ...), kind=kLoop, calls=%fused_computation.90 | loop fusion | flops 56623104 | bytes 47579136 | tf_op jit(solution)/shard_map/add | solution.py:57
  75.2 4.6 %collective-permute-start.7 = (f32[1,16,128,128]{3,2,1,0:T(8,128)S(1)}, f32[1,16,128,128]{3,2,1,0:T(8,128)S(1)}, u32[]{:S(2)}, u32[]{:S(2)}) collective-permute-start(f32[1,16,128,128]{3,2,1,0:T(8,128)S(1)} %get-tuple-element.57), channel_id=1, source_target_pairs={{32,0},{64,32},{96,64},{33,1},{65,33},{97,65},{34,2},{66,34},{98,6... | collective-permute-start | bytes 3145736 | tf_op jit(solution)/shard_map/ppermute | solution.py:18
  81.1 1.9 collective-permute-start.8
  83.0 3.6 %collective-permute-start.9 = (f32[8,1,128,128]{3,2,1,0:T(8,128)S(1)}, f32[8,1,128,128]{3,2,1,0:T(8,128)S(1)}, u32[]{:S(2)}, u32[]{:S(2)}) collective-permute-start(f32[8,1,128,128]{3,2,1,0:T(8,128)S(1)} %get-tuple-element.59), channel_id=1, source_target_pairs={{4,0},{8,4},{12,8},{16,12},{20,16},{24,20},{28,24},{5,1},{9,5},{13... | collective-permute-start | bytes 1572872 | tf_op jit(solution)/shard_map/ppermute | solution.py:18
  88.0 3.8 %collective-permute-start.10 = (f32[8,16,1,128]{3,2,1,0:T(1,128)S(1)}, f32[8,16,1,128]{3,2,1,0:T(1,128)S(1)}, u32[]{:S(2)}, u32[]{:S(2)}) collective-permute-start(f32[8,16,1,128]{3,2,1,0:T(1,128)S(1)} %get-tuple-element.54), channel_id=1, source_target_pairs={{0,1},{1,2},{2,3},{4,5},{5,6},{6,7},{8,9},{9,10},{10,11},{12,13},{... | collective-permute-start | bytes 196616 | tf_op jit(solution)/shard_map/ppermute | solution.py:17
  93.7 4.3 %collective-permute-done.11 = f32[8,16,1,128]{3,2,1,0:T(1,128)S(1)} collective-permute-done((f32[8,16,1,128]{3,2,1,0:T(1,128)S(1)}, f32[8,16,1,128]{3,2,1,0:T(1,128)S(1)}, u32[]{:S(2)}, u32[]{:S(2)}) %collective-permute-start.11) | collective-permute-done | bytes 65568 | tf_op jit(solution)/shard_map/ppermute | solution.py:18
  98.0 1.8 collective-permute-done.6
  101.0 28.2 %fusion.24 = f32[8,16,128,128]{3,2,1,0:T(8,128)} fusion(f32[8,16,128,128]{3,2,1,0:T(8,128)} %param.7, f32[8,16,1,128]{3,2,1,0:T(1,128)S(1)} %collective-permute-done.11, f32[10,1,128,128]{3,2,1,0:T(8,128)S(1)} %pad.55, f32[10,1,128,128]{3,2,1,0:T(8,128)S(1)} %pad.54, f32[1,16,128,128]{3,2,1,0:T(8,128)S(1)} %collective-permute-done.7, ...), kind=kLoop, calls=%fused_computation.62 | loop fusion | flops 73400320 | bytes 37093376 | tf_op jit(solution)/shard_map/add | solution.py:57
  132.2 5.1 %collective-permute-start.13 = (f32[1,16,128,128]{3,2,1,0:T(8,128)S(1)}, f32[1,16,128,128]{3,2,1,0:T(8,128)S(1)}, u32[]{:S(2)}, u32[]{:S(2)}) collective-permute-start(f32[1,16,128,128]{3,2,1,0:T(8,128)S(1)} %get-tuple-element.51), channel_id=1, source_target_pairs={{32,0},{64,32},{96,64},{33,1},{65,33},{97,65},{34,2},{66,34},{98,6... | collective-permute-start | bytes 3145736 | tf_op jit(solution)/shard_map/ppermute | solution.py:18
  138.6 1.9 collective-permute-start.14
  140.5 3.6 %collective-permute-start.15 = (f32[8,1,128,128]{3,2,1,0:T(8,128)S(1)}, f32[8,1,128,128]{3,2,1,0:T(8,128)S(1)}, u32[]{:S(2)}, u32[]{:S(2)}) collective-permute-start(f32[8,1,128,128]{3,2,1,0:T(8,128)S(1)} %get-tuple-element.53), channel_id=1, source_target_pairs={{4,0},{8,4},{12,8},{16,12},{20,16},{24,20},{28,24},{5,1},{9,5},{13... | collective-permute-start | bytes 1572872 | tf_op jit(solution)/shard_map/ppermute | solution.py:18
  145.5 3.8 %collective-permute-start.16 = (f32[8,16,1,128]{3,2,1,0:T(1,128)S(1)}, f32[8,16,1,128]{3,2,1,0:T(1,128)S(1)}, u32[]{:S(2)}, u32[]{:S(2)}) collective-permute-start(f32[8,16,1,128]{3,2,1,0:T(1,128)S(1)} %get-tuple-element.48), channel_id=1, source_target_pairs={{0,1},{1,2},{2,3},{4,5},{5,6},{6,7},{8,9},{9,10},{10,11},{12,13},{... | collective-permute-start | bytes 196616 | tf_op jit(solution)/shard_map/ppermute | solution.py:17
  151.2 4.3 %collective-permute-done.17 = f32[8,16,1,128]{3,2,1,0:T(1,128)S(1)} collective-permute-done((f32[8,16,1,128]{3,2,1,0:T(1,128)S(1)}, f32[8,16,1,128]{3,2,1,0:T(1,128)S(1)}, u32[]{:S(2)}, u32[]{:S(2)}) %collective-permute-start.17) | collective-permute-done | bytes 65568 | tf_op jit(solution)/shard_map/ppermute | solution.py:18
  157.6 28.2 %fusion.14 = f32[8,16,128,128]{3,2,1,0:T(8,128)} fusion(f32[8,16,128,128]{3,2,1,0:T(8,128)} %param.7, f32[8,16,1,128]{3,2,1,0:T(1,128)S(1)} %collective-permute-done.17, f32[10,1,128,128]{3,2,1,0:T(8,128)S(1)} %pad.59, f32[10,1,128,128]{3,2,1,0:T(8,128)S(1)} %pad.58, f32[1,16,128,128]{3,2,1,0:T(8,128)S(1)} %collective-permute-done.13, ...), kind=kLoop, calls=%fused_computation.34 | loop fusion | flops 73400320 | bytes 37093376 | tf_op jit(solution)/shard_map/add | solution.py:57
  188.8 5.1 %collective-permute-start.19 = (f32[1,16,128,128]{3,2,1,0:T(8,128)S(1)}, f32[1,16,128,128]{3,2,1,0:T(8,128)S(1)}, u32[]{:S(2)}, u32[]{:S(2)}) collective-permute-start(f32[1,16,128,128]{3,2,1,0:T(8,128)S(1)} %get-tuple-element.45), channel_id=1, source_target_pairs={{32,0},{64,32},{96,64},{33,1},{65,33},{97,65},{34,2},{66,34},{98,6... | collective-permute-start | bytes 3145736 | tf_op jit(solution)/shard_map/ppermute | solution.py:18
  195.2 1.9 collective-permute-start.20
  197.1 3.6 %collective-permute-start.21 = (f32[8,1,128,128]{3,2,1,0:T(8,128)S(1)}, f32[8,1,128,128]{3,2,1,0:T(8,128)S(1)}, u32[]{:S(2)}, u32[]{:S(2)}) collective-permute-start(f32[8,1,128,128]{3,2,1,0:T(8,128)S(1)} %get-tuple-element.47), channel_id=1, source_target_pairs={{4,0},{8,4},{12,8},{16,12},{20,16},{24,20},{28,24},{5,1},{9,5},{13... | collective-permute-start | bytes 1572872 | tf_op jit(solution)/shard_map/ppermute | solution.py:18
  202.1 3.8 %collective-permute-start.22 = (f32[8,16,1,128]{3,2,1,0:T(1,128)S(1)}, f32[8,16,1,128]{3,2,1,0:T(1,128)S(1)}, u32[]{:S(2)}, u32[]{:S(2)}) collective-permute-start(f32[8,16,1,128]{3,2,1,0:T(1,128)S(1)} %get-tuple-element.42), channel_id=1, source_target_pairs={{0,1},{1,2},{2,3},{4,5},{5,6},{6,7},{8,9},{9,10},{10,11},{12,13},{... | collective-permute-start | bytes 196616 | tf_op jit(solution)/shard_map/ppermute | solution.py:17
  207.8 4.3 %collective-permute-done.23 = f32[8,16,1,128]{3,2,1,0:T(1,128)S(1)} collective-permute-done((f32[8,16,1,128]{3,2,1,0:T(1,128)S(1)}, f32[8,16,1,128]{3,2,1,0:T(1,128)S(1)}, u32[]{:S(2)}, u32[]{:S(2)}) %collective-permute-start.23) | collective-permute-done | bytes 65568 | tf_op jit(solution)/shard_map/ppermute | solution.py:18
  213.4 28.2 %fusion.4 = f32[8,16,128,128]{3,2,1,0:T(8,128)} fusion(f32[8,16,128,128]{3,2,1,0:T(8,128)} %param.7, f32[8,16,1,128]{3,2,1,0:T(1,128)S(1)} %collective-permute-done.23, f32[10,1,128,128]{3,2,1,0:T(8,128)S(1)} %pad.63, f32[10,1,128,128]{3,2,1,0:T(8,128)S(1)} %pad.62, f32[1,16,128,128]{3,2,1,0:T(8,128)S(1)} %collective-permute-done.19, ...), kind=kLoop, calls=%fused_computation.6 | loop fusion | flops 73400320 | bytes 37093376 | tf_op jit(solution)/shard_map/add | solution.py:57
  241.6 8.5 %fusion.52 = f32[8,16,128,128]{3,2,1,0:T(8,128)} fusion(f32[8,16,128,128]{3,2,1,0:T(8,128)} %fusion.4), kind=kOutput, calls=%fused_computation.123 | output fusion | flops 14680064 | bytes 16777216 | tf_op jit(solution)/shard_map/jit(cumsum)/reduce_window_sum | solution.py:65
  250.1 2.3 slice.370
  252.4 50.6 %all-gather.3.cloned.1.call-done = f32[4,16,128,128]{3,2,1,0:T(8,128)} async-done(((f32[1,16,128,128]{3,2,1,0:T(8,128)}), f32[4,16,128,128]{3,2,1,0:T(8,128)}) %all-gather.3.cloned.1.call-update) | async-done | bytes 4194320 | tf_op jit(solution)/shard_map/all_gather | solution.py:31
  303.2 4.6 %while.10 = (s32[]{:T(128)}, f32[1,16,128,128]{3,2,1,0:T(8,128)S(1)}, s32[]{:T(128)}, f32[4,1,16,128,128]{4,3,2,1,0:T(8,128)}, s32[]{:T(128)}, /*index=5*/s32[]{:T(128)}, s32[]{:T(128)}) while((s32[]{:T(128)}, f32[1,16,128,128]{3,2,1,0:T(8,128)S(1)}, s32[]{:T(128)}, f32[4,1,16,128,128]{4,3,2,1,0:T(8,128)}, s32[]{:T(128)}, ...), condition=%wide.region_2.3_spmd, body=%wide.region_1.2_spmd.sunk | while | flops 262149 | bytes 3145843 | solution.py:37
  307.7 8.6 %add_multiply_fusion = f32[8,16,128,128]{3,2,1,0:T(8,128)} fusion(f32[8,16,128,128]{3,2,1,0:T(8,128)} %fusion.52, f32[16,128,128]{2,1,0:T(8,128)S(1)} %bitcast.11), kind=kLoop, calls=%fused_computation.107 | loop fusion | flops 4194304 | bytes 17825792 | tf_op jit(solution)/shard_map/div | solution.py:72
  (63 shorter events, 41.9 us)
Async XLA Ops:
  7.2 295.9 %all-gather.3.cloned.1.call-start = ((), (), s32[]{:S(2)}) async-start(), calls=%async_computation | async-start | bytes 5242880 | tf_op jit(solution)/shard_map/all_gather | solution.py:31
  7.2 30.0 %copy-start = (f32[8,16,128,128]{3,2,1,0:T(8,128)S(1)}, f32[8,16,128,128]{3,2,1,0:T(8,128)}, u32[]{:S(2)}) copy-start(f32[8,16,128,128]{3,2,1,0:T(8,128)} %param.5) | copy-start | bytes 25165828
  9.1 27.1 %collective-permute-start = (f32[1,16,128,128]{3,2,1,0:T(8,128)S(1)}, f32[1,16,128,128]{3,2,1,0:T(8,128)S(1)}, u32[]{:S(2)}, u32[]{:S(2)}) collective-permute-start(f32[1,16,128,128]{3,2,1,0:T(8,128)S(1)} %get-tuple-element.65), channel_id=1, source_target_pairs={{0,32},{32,64},{64,96},{1,33},{33,65},{65,97},{2,34},{34,66},{66,9... | collective-permute-start | bytes 3145736 | tf_op jit(solution)/shard_map/ppermute | solution.py:17
  10.6 31.3 %collective-permute-start.1 = (f32[1,16,128,128]{3,2,1,0:T(8,128)S(1)}, f32[1,16,128,128]{3,2,1,0:T(8,128)S(1)}, u32[]{:S(2)}, u32[]{:S(2)}) collective-permute-start(f32[1,16,128,128]{3,2,1,0:T(8,128)S(1)} %get-tuple-element.64), channel_id=1, source_target_pairs={{32,0},{64,32},{96,64},{33,1},{65,33},{97,65},{34,2},{66,34},{98,6... | collective-permute-start | bytes 3145736 | tf_op jit(solution)/shard_map/ppermute | solution.py:18
  16.5 10.7 %collective-permute-start.2 = (f32[8,1,128,128]{3,2,1,0:T(8,128)S(1)}, f32[8,1,128,128]{3,2,1,0:T(8,128)S(1)}, u32[]{:S(2)}, u32[]{:S(2)}) collective-permute-start(f32[8,1,128,128]{3,2,1,0:T(8,128)S(1)} %get-tuple-element.62), channel_id=1, source_target_pairs={{0,4},{4,8},{8,12},{12,16},{16,20},{20,24},{24,28},{1,5},{5,9},{9,... | collective-permute-start | bytes 1572872 | tf_op jit(solution)/shard_map/ppermute | solution.py:17
  18.5 11.0 %collective-permute-start.3 = (f32[8,1,128,128]{3,2,1,0:T(8,128)S(1)}, f32[8,1,128,128]{3,2,1,0:T(8,128)S(1)}, u32[]{:S(2)}, u32[]{:S(2)}) collective-permute-start(f32[8,1,128,128]{3,2,1,0:T(8,128)S(1)} %get-tuple-element.63), channel_id=1, source_target_pairs={{4,0},{8,4},{12,8},{16,12},{20,16},{24,20},{28,24},{5,1},{9,5},{13... | collective-permute-start | bytes 1572872 | tf_op jit(solution)/shard_map/ppermute | solution.py:18
  23.4 20.6 %collective-permute-start.4 = (f32[8,16,1,128]{3,2,1,0:T(1,128)S(1)}, f32[8,16,1,128]{3,2,1,0:T(1,128)S(1)}, u32[]{:S(2)}, u32[]{:S(2)}) collective-permute-start(f32[8,16,1,128]{3,2,1,0:T(1,128)S(1)} %get-tuple-element.60), channel_id=1, source_target_pairs={{0,1},{1,2},{2,3},{4,5},{5,6},{6,7},{8,9},{9,10},{10,11},{12,13},{... | collective-permute-start | bytes 196616 | tf_op jit(solution)/shard_map/ppermute | solution.py:17
  27.3 16.7 %collective-permute-start.5 = (f32[8,16,1,128]{3,2,1,0:T(1,128)S(1)}, f32[8,16,1,128]{3,2,1,0:T(1,128)S(1)}, u32[]{:S(2)}, u32[]{:S(2)}) collective-permute-start(f32[8,16,1,128]{3,2,1,0:T(1,128)S(1)} %get-tuple-element.61), channel_id=1, source_target_pairs={{1,0},{2,1},{3,2},{5,4},{6,5},{7,6},{9,8},{10,9},{11,10},{13,12},{... | collective-permute-start | bytes 196616 | tf_op jit(solution)/shard_map/ppermute | solution.py:18
  36.1 7.9 %slice-start = ((s8[8388608]{0:T(1024)(128)(4,1)}), s8[4194304]{0:T(1024)(128)(4,1)S(1)}, s32[]{:S(2)}) async-start(s8[8388608]{0:T(1024)(128)(4,1)} %bitcast.9), calls=%async_computation.1 | async-start | bytes 8388608
  37.2 6.8 %slice-start.1 = ((s8[8388608]{0:T(1024)(128)(4,1)}), s8[4194304]{0:T(1024)(128)(4,1)S(1)}, s32[]{:S(2)}) async-start(s8[8388608]{0:T(1024)(128)(4,1)} %bitcast.9), calls=%async_computation.2 | async-start | bytes 8388608
  42.0 1.0 copy-start.1
  73.9 25.9 %collective-permute-start.6 = (f32[1,16,128,128]{3,2,1,0:T(8,128)S(1)}, f32[1,16,128,128]{3,2,1,0:T(8,128)S(1)}, u32[]{:S(2)}, u32[]{:S(2)}) collective-permute-start(f32[1,16,128,128]{3,2,1,0:T(8,128)S(1)} %get-tuple-element.56), channel_id=1, source_target_pairs={{0,32},{32,64},{64,96},{1,33},{33,65},{65,97},{2,34},{34,66},{66,9... | collective-permute-start | bytes 3145736 | tf_op jit(solution)/shard_map/ppermute | solution.py:17
  75.2 25.8 %collective-permute-start.7 = (f32[1,16,128,128]{3,2,1,0:T(8,128)S(1)}, f32[1,16,128,128]{3,2,1,0:T(8,128)S(1)}, u32[]{:S(2)}, u32[]{:S(2)}) collective-permute-start(f32[1,16,128,128]{3,2,1,0:T(8,128)S(1)} %get-tuple-element.57), channel_id=1, source_target_pairs={{32,0},{64,32},{96,64},{33,1},{65,33},{97,65},{34,2},{66,34},{98,6... | collective-permute-start | bytes 3145736 | tf_op jit(solution)/shard_map/ppermute | solution.py:18
  81.1 10.7 %collective-permute-start.8 = (f32[8,1,128,128]{3,2,1,0:T(8,128)S(1)}, f32[8,1,128,128]{3,2,1,0:T(8,128)S(1)}, u32[]{:S(2)}, u32[]{:S(2)}) collective-permute-start(f32[8,1,128,128]{3,2,1,0:T(8,128)S(1)} %get-tuple-element.58), channel_id=1, source_target_pairs={{0,4},{4,8},{8,12},{12,16},{16,20},{20,24},{24,28},{1,5},{5,9},{9,... | collective-permute-start | bytes 1572872 | tf_op jit(solution)/shard_map/ppermute | solution.py:17
  83.0 10.3 %collective-permute-start.9 = (f32[8,1,128,128]{3,2,1,0:T(8,128)S(1)}, f32[8,1,128,128]{3,2,1,0:T(8,128)S(1)}, u32[]{:S(2)}, u32[]{:S(2)}) collective-permute-start(f32[8,1,128,128]{3,2,1,0:T(8,128)S(1)} %get-tuple-element.59), channel_id=1, source_target_pairs={{4,0},{8,4},{12,8},{16,12},{20,16},{24,20},{28,24},{5,1},{9,5},{13... | collective-permute-start | bytes 1572872 | tf_op jit(solution)/shard_map/ppermute | solution.py:18
  88.0 5.7 %collective-permute-start.10 = (f32[8,16,1,128]{3,2,1,0:T(1,128)S(1)}, f32[8,16,1,128]{3,2,1,0:T(1,128)S(1)}, u32[]{:S(2)}, u32[]{:S(2)}) collective-permute-start(f32[8,16,1,128]{3,2,1,0:T(1,128)S(1)} %get-tuple-element.54), channel_id=1, source_target_pairs={{0,1},{1,2},{2,3},{4,5},{5,6},{6,7},{8,9},{9,10},{10,11},{12,13},{... | collective-permute-start | bytes 196616 | tf_op jit(solution)/shard_map/ppermute | solution.py:17
  91.8 6.2 %collective-permute-start.11 = (f32[8,16,1,128]{3,2,1,0:T(1,128)S(1)}, f32[8,16,1,128]{3,2,1,0:T(1,128)S(1)}, u32[]{:S(2)}, u32[]{:S(2)}) collective-permute-start(f32[8,16,1,128]{3,2,1,0:T(1,128)S(1)} %get-tuple-element.55), channel_id=1, source_target_pairs={{1,0},{2,1},{3,2},{5,4},{6,5},{7,6},{9,8},{10,9},{11,10},{13,12},{... | collective-permute-start | bytes 196616 | tf_op jit(solution)/shard_map/ppermute | solution.py:18
  130.9 25.6 %collective-permute-start.12 = (f32[1,16,128,128]{3,2,1,0:T(8,128)S(1)}, f32[1,16,128,128]{3,2,1,0:T(8,128)S(1)}, u32[]{:S(2)}, u32[]{:S(2)}) collective-permute-start(f32[1,16,128,128]{3,2,1,0:T(8,128)S(1)} %get-tuple-element.50), channel_id=1, source_target_pairs={{0,32},{32,64},{64,96},{1,33},{33,65},{65,97},{2,34},{34,66},{66,9... | collective-permute-start | bytes 3145736 | tf_op jit(solution)/shard_map/ppermute | solution.py:17
  132.2 25.4 %collective-permute-start.13 = (f32[1,16,128,128]{3,2,1,0:T(8,128)S(1)}, f32[1,16,128,128]{3,2,1,0:T(8,128)S(1)}, u32[]{:S(2)}, u32[]{:S(2)}) collective-permute-start(f32[1,16,128,128]{3,2,1,0:T(8,128)S(1)} %get-tuple-element.51), channel_id=1, source_target_pairs={{32,0},{64,32},{96,64},{33,1},{65,33},{97,65},{34,2},{66,34},{98,6... | collective-permute-start | bytes 3145736 | tf_op jit(solution)/shard_map/ppermute | solution.py:18
  138.6 10.7 %collective-permute-start.14 = (f32[8,1,128,128]{3,2,1,0:T(8,128)S(1)}, f32[8,1,128,128]{3,2,1,0:T(8,128)S(1)}, u32[]{:S(2)}, u32[]{:S(2)}) collective-permute-start(f32[8,1,128,128]{3,2,1,0:T(8,128)S(1)} %get-tuple-element.52), channel_id=1, source_target_pairs={{0,4},{4,8},{8,12},{12,16},{16,20},{20,24},{24,28},{1,5},{5,9},{9,... | collective-permute-start | bytes 1572872 | tf_op jit(solution)/shard_map/ppermute | solution.py:17
  140.5 10.3 %collective-permute-start.15 = (f32[8,1,128,128]{3,2,1,0:T(8,128)S(1)}, f32[8,1,128,128]{3,2,1,0:T(8,128)S(1)}, u32[]{:S(2)}, u32[]{:S(2)}) collective-permute-start(f32[8,1,128,128]{3,2,1,0:T(8,128)S(1)} %get-tuple-element.53), channel_id=1, source_target_pairs={{4,0},{8,4},{12,8},{16,12},{20,16},{24,20},{28,24},{5,1},{9,5},{13... | collective-permute-start | bytes 1572872 | tf_op jit(solution)/shard_map/ppermute | solution.py:18
  145.5 5.7 %collective-permute-start.16 = (f32[8,16,1,128]{3,2,1,0:T(1,128)S(1)}, f32[8,16,1,128]{3,2,1,0:T(1,128)S(1)}, u32[]{:S(2)}, u32[]{:S(2)}) collective-permute-start(f32[8,16,1,128]{3,2,1,0:T(1,128)S(1)} %get-tuple-element.48), channel_id=1, source_target_pairs={{0,1},{1,2},{2,3},{4,5},{5,6},{6,7},{8,9},{9,10},{10,11},{12,13},{... | collective-permute-start | bytes 196616 | tf_op jit(solution)/shard_map/ppermute | solution.py:17
  149.3 6.2 %collective-permute-start.17 = (f32[8,16,1,128]{3,2,1,0:T(1,128)S(1)}, f32[8,16,1,128]{3,2,1,0:T(1,128)S(1)}, u32[]{:S(2)}, u32[]{:S(2)}) collective-permute-start(f32[8,16,1,128]{3,2,1,0:T(1,128)S(1)} %get-tuple-element.49), channel_id=1, source_target_pairs={{1,0},{2,1},{3,2},{5,4},{6,5},{7,6},{9,8},{10,9},{11,10},{13,12},{... | collective-permute-start | bytes 196616 | tf_op jit(solution)/shard_map/ppermute | solution.py:18
  187.5 24.7 %collective-permute-start.18 = (f32[1,16,128,128]{3,2,1,0:T(8,128)S(1)}, f32[1,16,128,128]{3,2,1,0:T(8,128)S(1)}, u32[]{:S(2)}, u32[]{:S(2)}) collective-permute-start(f32[1,16,128,128]{3,2,1,0:T(8,128)S(1)} %get-tuple-element.44), channel_id=1, source_target_pairs={{0,32},{32,64},{64,96},{1,33},{33,65},{65,97},{2,34},{34,66},{66,9... | collective-permute-start | bytes 3145736 | tf_op jit(solution)/shard_map/ppermute | solution.py:17
  188.8 24.6 %collective-permute-start.19 = (f32[1,16,128,128]{3,2,1,0:T(8,128)S(1)}, f32[1,16,128,128]{3,2,1,0:T(8,128)S(1)}, u32[]{:S(2)}, u32[]{:S(2)}) collective-permute-start(f32[1,16,128,128]{3,2,1,0:T(8,128)S(1)} %get-tuple-element.45), channel_id=1, source_target_pairs={{32,0},{64,32},{96,64},{33,1},{65,33},{97,65},{34,2},{66,34},{98,6... | collective-permute-start | bytes 3145736 | tf_op jit(solution)/shard_map/ppermute | solution.py:18
  195.2 10.7 %collective-permute-start.20 = (f32[8,1,128,128]{3,2,1,0:T(8,128)S(1)}, f32[8,1,128,128]{3,2,1,0:T(8,128)S(1)}, u32[]{:S(2)}, u32[]{:S(2)}) collective-permute-start(f32[8,1,128,128]{3,2,1,0:T(8,128)S(1)} %get-tuple-element.46), channel_id=1, source_target_pairs={{0,4},{4,8},{8,12},{12,16},{16,20},{20,24},{24,28},{1,5},{5,9},{9,... | collective-permute-start | bytes 1572872 | tf_op jit(solution)/shard_map/ppermute | solution.py:17
  197.1 10.3 %collective-permute-start.21 = (f32[8,1,128,128]{3,2,1,0:T(8,128)S(1)}, f32[8,1,128,128]{3,2,1,0:T(8,128)S(1)}, u32[]{:S(2)}, u32[]{:S(2)}) collective-permute-start(f32[8,1,128,128]{3,2,1,0:T(8,128)S(1)} %get-tuple-element.47), channel_id=1, source_target_pairs={{4,0},{8,4},{12,8},{16,12},{20,16},{24,20},{28,24},{5,1},{9,5},{13... | collective-permute-start | bytes 1572872 | tf_op jit(solution)/shard_map/ppermute | solution.py:18
  202.1 5.7 %collective-permute-start.22 = (f32[8,16,1,128]{3,2,1,0:T(1,128)S(1)}, f32[8,16,1,128]{3,2,1,0:T(1,128)S(1)}, u32[]{:S(2)}, u32[]{:S(2)}) collective-permute-start(f32[8,16,1,128]{3,2,1,0:T(1,128)S(1)} %get-tuple-element.42), channel_id=1, source_target_pairs={{0,1},{1,2},{2,3},{4,5},{5,6},{6,7},{8,9},{9,10},{10,11},{12,13},{... | collective-permute-start | bytes 196616 | tf_op jit(solution)/shard_map/ppermute | solution.py:17
  205.9 6.2 %collective-permute-start.23 = (f32[8,16,1,128]{3,2,1,0:T(1,128)S(1)}, f32[8,16,1,128]{3,2,1,0:T(1,128)S(1)}, u32[]{:S(2)}, u32[]{:S(2)}) collective-permute-start(f32[8,16,1,128]{3,2,1,0:T(1,128)S(1)} %get-tuple-element.43), channel_id=1, source_target_pairs={{1,0},{2,1},{3,2},{5,4},{6,5},{7,6},{9,8},{10,9},{11,10},{13,12},{... | collective-permute-start | bytes 196616 | tf_op jit(solution)/shard_map/ppermute | solution.py:18
Sparse Core Ops, SparseCore 0:
  252.5 50.4 all-gather.2
where the time goes:
time: 324 us; the launch traced here: 323 us
  other arithmetic  134 us (41%)
  waiting for transfers between devices  77 us (24%)
  starting transfers between devices  67.8 us (21%)
  local copies, waits for them, and re-layouts  29.6 us (9%)
  between operations  14.4 us (4%)
    add x4, other arithmetic, one_step(): return 2.0 * middle - before + speed_square * spread  113 us
    all_gather x1, waiting for transfers between devices, prefix(): gathered = lax.all_gather(part, axis)  50.6 us
    ppermute x12, starting transfers between devices, with_halo(): lax.ppermute(initial, axis, [(b, a) for a, b in up])  39.3 us
    ppermute x12, starting transfers between devices, with_halo(): lax.ppermute(last, axis, up)  28.4 us
    ppermute x12, waiting for transfers between devices, with_halo(): lax.ppermute(initial, axis, [(b, a) for a, b in up])  16.8 us
    slice x11, local copies, waits for them, and re-layouts, with_halo(): last = lax.slice_in_dim(array, length - width, length, axis=dim)  15.4 us
    ppermute x12, waiting for transfers between devices, with_halo(): lax.ppermute(last, axis, up)  9.54 us
    div x1, other arithmetic, shards(): (here + below) / (field_now.shape[0] * lax.axis_size('south'))  8.62 us
  transfers between devices with their start and end apart: 25, of which 16 were waited for; matrix products, arithmetic and copies ran while one was open for 6% of the time, Pallas kernels for 0%

commit v1 on v0

v1 whole, which is shorter than its diff:
```python
import jax
import jax.numpy as jnp
from jax import lax
from jax.experimental import pallas as pl
from jax.experimental.pallas import tpu as pltpu
from jax.sharding import PartitionSpec as P


STEPS = 4
PAD = 8
ROWS = 32
MIB = 1 << 20


VM = pl.BlockSpec(memory_space=pltpu.VMEM)
HBM = pl.BlockSpec(memory_space=pltpu.HBM)


def call(body, ins, outs, out_specs, in_specs, alias=None, scratch=(), limit=6, flops=0, moved=0):
    return pl.pallas_call(
        body,
        out_shape=outs,
        in_specs=in_specs,
        out_specs=out_specs,
        scratch_shapes=scratch,
        input_output_aliases=alias or {},
        compiler_params=pltpu.CompilerParams(vmem_limit_bytes=limit * MIB),
        cost_estimate=pl.CostEstimate(flops=flops, bytes_accessed=moved, transcendentals=0),
    )(*ins)


def vmem(shape):
    return pltpu.VMEM(shape, jnp.float32)


def copy_all(copies):
    for copy in copies:
        copy.start()
    for copy in copies:
        copy.wait()


def ring(count, step):
    pairs = [(i, i + 1) for i in range(count - 1)]
    return pairs if step > 0 else [(b, a) for a, b in pairs]


def cell_rows(now, before, speed, j, i, k, jm, jp, im, ip):
    at = PAD + k
    mid = now[j, i, pl.ds(at, ROWS), :]
    spread = jm(k) + jp(k) + im(k) + ip(k)
    spread = spread + now[j, i, pl.ds(at - 1, ROWS), :] + now[j, i, pl.ds(at + 1, ROWS), :] - 6.0 * mid
    return 2.0 * mid - before[j, i, pl.ds(at, ROWS), :] + speed[j, i, pl.ds(k, ROWS), :] * spread


def inside(ref, j, i):
    return lambda k: ref[j, i, pl.ds(PAD + k, ROWS), :]


def face(ref, n):
    return lambda k: ref[n, pl.ds(k, ROWS), :]


def columns(now, before, speed, j, i, low_i, high_i, halo, put):
    jm, jp = halo
    for k in range(0, speed.shape[2], ROWS):
        new = cell_rows(now, before, speed, j, i, k, jm, jp, low_i, high_i)
        before[j, i, pl.ds(PAD + k, ROWS), :] = new
        for ref, n in put:
            ref[n, pl.ds(k, ROWS), :] = new


def solution(mesh):
    south, east, down = (mesh.shape[a] for a in ("south", "east", "down"))

    def shards(field_now, earlier, speed_square):
        nj, ni, nk, nm = field_now.shape
        half = ni // 2
        padded = (nj, ni, nk + 2 * PAD, nm)
        xs, ys, zs = (half, nk, nm), (nj, nk, nm), (nj, ni, nm)
        cells = half * nj * nk * nm

        def send(value, axis, count, step):
            return lax.ppermute(value, axis, ring(count, step))

        field_now, earlier, speed_square = (
            pltpu.with_memory_space_constraint(v, pltpu.HBM) for v in (field_now, earlier, speed_square)
        )

        def faces_body(field, xau, xad, xbu, xbd, yu, yd, sem):
            pairs = [
                (field.at[nj - 1, pl.ds(0, half)], xau),
                (field.at[0, pl.ds(0, half)], xad),
                (field.at[nj - 1, pl.ds(half, half)], xbu),
                (field.at[0, pl.ds(half, half)], xbd),
                (field.at[:, ni - 1], yu),
                (field.at[:, 0], yd),
            ]
            copy_all([pltpu.make_async_copy(a, b, sem.at[n]) for n, (a, b) in enumerate(pairs)])

        xau, xad, xbu, xbd, yu, yd = call(
            faces_body, [field_now],
            [vmem(xs)] * 4 + [vmem(ys)] * 2, [VM] * 6, [HBM],
            scratch=[pltpu.SemaphoreType.DMA((6,))], flops=1000, moved=6 * MIB,
        )

        def load_body(field, before, speed, now, prev, c, zu, zd, sem):
            copies = [
                pltpu.make_async_copy(field, now.at[:, :, pl.ds(PAD, nk)], sem.at[0]),
                pltpu.make_async_copy(before, prev.at[:, :, pl.ds(PAD, nk)], sem.at[1]),
                pltpu.make_async_copy(speed, c, sem.at[2]),
            ]
            for copy in copies:
                copy.start()
            copies[0].wait()
            z_faces(now, zu, zd)
            copies[1].wait()
            copies[2].wait()

        def z_faces(ref, zu, zd):
            def one(j, carry):
                for i in range(ni):
                    zd[j, pl.ds(i, 1), :] = ref[j, i, pl.ds(PAD, 1), :]
                    zu[j, pl.ds(i, 1), :] = ref[j, i, pl.ds(PAD + nk - 1, 1), :]
                return carry

            lax.fori_loop(0, nj, one, 0)

        now, prev, c, zu, zd = call(
            load_body, [field_now, earlier, speed_square],
            [vmem(padded), vmem(padded), vmem(field_now.shape), vmem(zs), vmem(zs)],
            [VM] * 5, [HBM] * 3,
            scratch=[pltpu.SemaphoreType.DMA((3,))], flops=40000000, moved=48 * MIB,
        )

        def row_ends(now, j, i, y_low, y_high):
            low = face(y_low, j) if isinstance(i, int) and i == 0 else inside(now, j, i - 1)
            high = face(y_high, j) if isinstance(i, int) and i == ni - 1 else inside(now, j, i + 1)
            return low, high

        def j_ends(now, j, i, x_low, x_high, first):
            if isinstance(j, int) and j == 0:
                return face(x_low, i - first), inside(now, 1, i)
            if isinstance(j, int) and j == nj - 1:
                return inside(now, nj - 2, i), face(x_high, i - first)
            return inside(now, j - 1, i), inside(now, j + 1, i)

        def edge_body(part):
            first = part * half
            outer = 0 if part == 0 else ni - 1
            inner = range(1, half) if part == 0 else range(half, ni - 1)

            def body(*refs):
                if part == 0:
                    now, before, speed, x_low, x_high, y_face, z_low, z_high = refs[:8]
                    now_out, out, xu, xd, yo = refs[8:]

                    def pads(j, carry):
                        for i in range(ni):
                            now_out[j, i, pl.ds(PAD - 1, 1), :] = z_low[j, pl.ds(i, 1), :]
                            now_out[j, i, pl.ds(PAD + nk, 1), :] = z_high[j, pl.ds(i, 1), :]
                        return carry

                    lax.fori_loop(0, nj, pads, 0)
                    now = now_out
                else:
                    now, before, speed, x_low, x_high, y_face = refs[:6]
                    out, xu, xd, yo = refs[6:]
                for j, x_out in ((0, xd), (nj - 1, xu)):
                    low, high = row_ends(now, j, outer, y_face, y_face)
                    columns(now, out, speed, j, outer, low, high, j_ends(now, j, outer, x_low, x_high, first),
                            [(x_out, outer - first), (yo, j)])

                    def one(i, carry, j=j, x_out=x_out):
                        low, high = row_ends(now, j, i, None, None)
                        columns(now, out, speed, j, i, low, high, j_ends(now, j, i, x_low, x_high, first),
                                [(x_out, i - first)])
                        return carry

                    lax.fori_loop(inner.start, inner.stop, one, 0)

                def side(j, carry):
                    low, high = row_ends(now, j, outer, y_face, y_face)
                    columns(now, out, speed, j, outer, low, high, j_ends(now, j, outer, None, None, first), [(yo, j)])
                    return carry

                lax.fori_loop(1, nj - 1, side, 0)

            return body

        def bulk_body(part):
            inner = range(1, half) if part == 0 else range(half, ni - 1)
            count = len(inner)

            def body(*refs):
                now, _, speed, out = refs[:4]

                def one(n, carry):
                    j, i = 1 + n // count, inner.start + n % count
                    low, high = row_ends(now, j, i, None, None)
                    columns(now, out, speed, j, i, low, high, j_ends(now, j, i, None, None, 0), [])
                    return carry

                lax.fori_loop(0, (nj - 2) * count, one, 0)
                if part == 1:
                    z_faces(out, *refs[4:])

            return body

        def last_body(part):
            first = part * half

            def body(*refs):
                if part == 0:
                    now, before, speed, x_low, x_high, y_face, z_low, z_high = refs[:8]
                    now_out, out, total = refs[8:]

                    def pads(j, carry):
                        for i in range(ni):
                            now_out[j, i, pl.ds(PAD - 1, 1), :] = z_low[j, pl.ds(i, 1), :]
                            now_out[j, i, pl.ds(PAD + nk, 1), :] = z_high[j, pl.ds(i, 1), :]
                        return carry

                    lax.fori_loop(0, nj, pads, 0)
                    now = now_out
                else:
                    now, before, speed, x_low, x_high, y_face = refs[:6]
                    out, total = refs[6:]

                def row(i):
                    for k in range(0, nk, ROWS):
                        acc = None
                        for j in range(nj):
                            low, high = row_ends(now, j, i, y_face, y_face)
                            jm, jp = j_ends(now, j, i, x_low, x_high, first)
                            new = cell_rows(now, out, speed, j, i, k, jm, jp, low, high)
                            out[j, i, pl.ds(PAD + k, ROWS), :] = new
                            acc = new if acc is None else acc + new
                        total[i - first, pl.ds(k, ROWS), :] = acc

                def one(i, carry):
                    row(i)
                    return carry

                if part == 0:
                    row(0)
                    lax.fori_loop(1, half, one, 0)
                else:
                    lax.fori_loop(half, ni - 1, one, 0)
                    row(ni - 1)

            return body

        def running_body(part):
            first = part * half
            scale = 1.0 / (nj * south)

            def body(*refs):
                u, p, q, r = refs[:4]
                result, buffer, sem = refs[-3:]

                def copy(i):
                    return pltpu.make_async_copy(buffer.at[:, i], result.at[:, first + i], sem)

                def one(i, carry):
                    for k in range(0, nk, ROWS):
                        rows = pl.ds(k, ROWS)
                        acc = p[i, rows, :] + q[i, rows, :] + r[i, rows, :]
                        for j in range(nj):
                            acc = acc + u[j, first + i, pl.ds(PAD + k, ROWS), :]
                            buffer[j, i, rows, :] = acc * scale
                    copy(i).start()
                    return carry

                lax.fori_loop(0, half, one, 0)
                pltpu.make_async_copy(buffer, result.at[:, pl.ds(first, half)], sem).wait()

            return body

        def store_body(u, result, sem):
            copy_all([pltpu.make_async_copy(u.at[:, :, pl.ds(PAD, nk)], result, sem)])

        a_low, a_high = send(xau, "south", south, 1), send(xad, "south", south, -1)
        y_low, y_high = send(yu, "east", east, 1), send(yd, "east", east, -1)
        b_low, b_high = send(xbu, "south", south, 1), send(xbd, "south", south, -1)
        z_low, z_high = send(zu, "down", down, 1), send(zd, "down", down, -1)

        for _ in range(STEPS - 1):
            now, prev, xau, xad, yd = call(
                edge_body(0),
                [now, prev, c, a_low, a_high, y_low, z_low, z_high],
                [vmem(padded), vmem(padded), vmem(xs), vmem(xs), vmem(ys)], [VM] * 5, [VM] * 8,
                alias={0: 0, 1: 1}, flops=3 * cells, moved=3 * MIB,
            )
            a_low, a_high = send(xau, "south", south, 1), send(xad, "south", south, -1)
            new_y_high = send(yd, "east", east, -1)
            prev = call(
                bulk_body(0), [now, prev, c], vmem(padded), VM, [VM] * 3,
                alias={1: 0}, flops=9 * cells, moved=8 * MIB,
            )
            prev, xbu, xbd, yu = call(
                edge_body(1),
                [now, prev, c, b_low, b_high, y_high],
                [vmem(padded), vmem(xs), vmem(xs), vmem(ys)], [VM] * 4, [VM] * 6,
                alias={1: 0}, flops=3 * cells, moved=3 * MIB,
            )
            y_low = send(yu, "east", east, 1)
            b_low, b_high = send(xbu, "south", south, 1), send(xbd, "south", south, -1)
            prev, zu, zd = call(
                bulk_body(1), [now, prev, c],
                [vmem(padded), vmem(zs), vmem(zs)], [VM] * 3, [VM] * 3,
                alias={1: 0}, flops=9 * cells, moved=8 * MIB,
            )
            z_low, z_high = send(zu, "down", down, 1), send(zd, "down", down, -1)
            y_high = new_y_high
            now, prev = prev, now

        def first_round(total):
            p = lax.ppermute(total, "south", [(0, 1), (1, 2)])
            return p, lax.ppermute(total, "south", [(0, 3)])

        def second_round(total, p, q):
            def body(total, p, q, out):
                last = lax.axis_index("south") == 3
                for i in range(half):
                    out[i] = jnp.where(last, q[i], total[i] + p[i])

            value = call(body, [total, p, q], vmem(xs), VM, [VM] * 3, flops=half * nk * nm, moved=2 * MIB)
            return lax.ppermute(value, "south", [(2, 3), (3, 2)])

        now, prev, total_a = call(
            last_body(0), [now, prev, c, a_low, a_high, y_low, z_low, z_high],
            [vmem(padded), vmem(padded), vmem(xs)], [VM] * 3, [VM] * 8,
            alias={0: 0, 1: 1}, flops=12 * cells, moved=12 * MIB,
        )
        pa, qa = first_round(total_a)
        prev, total_b = call(
            last_body(1), [now, prev, c, b_low, b_high, y_high],
            [vmem(padded), vmem(xs)], [VM] * 2, [VM] * 6,
            alias={1: 0}, flops=12 * cells, moved=12 * MIB,
        )
        pb, qb = first_round(total_b)
        end = call(
            store_body, [prev], jax.ShapeDtypeStruct(field_now.shape, jnp.float32), HBM, [VM],
            scratch=[pltpu.SemaphoreType.DMA], flops=10000000, moved=16 * MIB,
        )
        ra = second_round(total_a, pa, qa)
        rb = second_round(total_b, pb, qb)
        shape = jax.ShapeDtypeStruct(field_now.shape, jnp.float32)
        scratch = [pltpu.VMEM((nj, half, nk, nm), jnp.float32), pltpu.SemaphoreType.DMA]
        running = call(
            running_body(0), [prev, pa, qa, ra], shape, HBM, [VM] * 4,
            scratch=scratch, limit=10, flops=2 * cells, moved=8 * MIB,
        )
        running = call(
            running_body(1), [prev, pb, qb, rb, running], shape, HBM, [VM] * 4 + [HBM],
            alias={4: 0}, scratch=scratch, limit=10, flops=2 * cells, moved=8 * MIB,
        )
        return running, end

    spec = P("south", "east", "down", None)
    return jax.shard_map(shards, mesh=mesh, in_specs=(spec,) * 3, out_specs=(spec, spec), check_vma=False)
```

time: 324 us -> 188 us (0.58)
  other arithmetic: 134 us -> 0 us
  Pallas kernels: 0 us -> 39.5 us
  starting transfers between devices: 67.8 us -> 103 us
  waiting for transfers between devices: 77 us -> 41.8 us
  local copies, waits for them, and re-layouts: 29.6 us -> 0 us
  between operations: 14.4 us -> 1.22 us
    add x7 -> x0, other arithmetic: 117 us -> none  [the longest x4 113 us: one_step(): return 2.0 * middle - before + speed_square * spread]
    all_gather x1 -> x0, waiting for transfers between devices: 50.6 us -> none  [prefix(): gathered = lax.all_gather(part, axis)]
    pallas_call x0 -> x21, Pallas kernels: none -> 39.5 us  [call(): pl.pallas_call(body, out_shape=outs, in_specs=in_specs, out_specs=out_spe...]
    ppermute x24 -> x38, starting transfers between devices: 67.7 us -> 103 us  [the longest x32 86.6 us: send(): return lax.ppermute(value, axis, ring(count, step))]
    slice x13 -> x0, local copies, waits for them, and re-layouts: 19.6 us -> none  [the longest x11 15.4 us: with_halo(): last = lax.slice_in_dim(array, length - width, length, axis=dim)]
    ppermute x24 -> x38, waiting for transfers between devices: 26.3 us -> 41.8 us  [the longest x32 29.1 us: send(): return lax.ppermute(value, axis, ring(count, step))]
    div x1 -> x0, other arithmetic: 8.62 us -> none  [shards(): (here + below) / (field_now.shape[0] * lax.axis_size('south'))]
    another operation x1 -> x0, other arithmetic: 8.46 us -> none  [shards(): here = jnp.cumsum(field_now, axis=0)]
  transfers between devices with their start and end apart: 25 -> 38, of which waited for: 16 -> 15; matrix products, arithmetic and copies ran while one was open for 6% -> 0% of each run, Pallas kernels for 0% -> 19%
where the time goes in v1:
time: 188 us; the launch traced here: 185 us
  starting transfers between devices  103 us (55%)
  waiting for transfers between devices  41.8 us (22%)
  Pallas kernels  39.5 us (21%)
    ppermute x32, starting transfers between devices, send(): return lax.ppermute(value, axis, ring(count, step))  86.6 us
    pallas_call x21, Pallas kernels, call(): pl.pallas_call(body, out_shape=outs, in_specs=in_specs, out_specs=out_spe...  39.5 us
    ppermute x32, waiting for transfers between devices, send(): return lax.ppermute(value, axis, ring(count, step))  29.1 us
    ppermute x2, starting transfers between devices, second_round(): return lax.ppermute(value, 'south', [(2, 3), (3, 2)])  12.3 us
    ppermute x2, waiting for transfers between devices, first_round(): return (p, lax.ppermute(total, 'south', [(0, 3)]))  8.12 us
    ppermute x2, waiting for transfers between devices, second_round(): return lax.ppermute(value, 'south', [(2, 3), (3, 2)])  4.51 us
  transfers between devices with their start and end apart: 38, of which 15 were waited for; matrix products, arithmetic and copies ran while one was open for 0% of the time, Pallas kernels for 19%

profile of v1, /device:TPU:14, one launch (start us, length us, event | category | flops | bytes accessed | tf_op | source)
XLA Modules:
  0.0 185.4 jit_solution(10415090965183992898)
XLA Ops:
  3.8 8.2 %shard_map.50 = (f32[8,16,144,128]{3,2,1,0:T(8,128)S(1)}, f32[8,16,144,128]{3,2,1,0:T(8,128)S(1)}, f32[8,16,128,128]{3,2,1,0:T(8,128)S(1)}, f32[8,16,128]{2,1,0:T(8,128)S(1)}, f32[8,16,128]{2,1,0:T(8,128)S(1)}) custom-call(f32[8,16,128,128]{3,2,1,0:T(8,128)} %field.3, f32[8,16,128,128]{3,2,1,0:T(8,128)} %before.1, f32[8,16,128,128]{3,2,1,0:T(8,128)} %speed.1), custom_call_target="tpu_custom_call" | custom-call | flops 40000000 | bytes 50331648 | tf_op jit(solution)/shard_map/pallas_call | solution.py:20
  12.0 3.8 %collective-permute-start.3 = (f32[8,16,128]{2,1,0:T(8,128)S(1)}, f32[8,16,128]{2,1,0:T(8,128)S(1)}, u32[]{:S(2)}, u32[]{:S(2)}) collective-permute-start(f32[8,16,128]{2,1,0:T(8,128)S(1)} %get-tuple-element.60), channel_id=1, source_target_pairs={{0,1},{1,2},{2,3},{4,5},{5,6},{6,7},{8,9},{9,10},{10,11},{12,13},{... | collective-permute-start | bytes 196616 | tf_op jit(solution)/shard_map/ppermute | solution.py:84
  17.1 4.6 %collective-permute-start.1 = (f32[8,128,128]{2,1,0:T(8,128)S(1)}, f32[8,128,128]{2,1,0:T(8,128)S(1)}, u32[]{:S(2)}, u32[]{:S(2)}) collective-permute-start(f32[8,128,128]{2,1,0:T(8,128)S(1)} %get-tuple-element.58), channel_id=1, source_target_pairs={{32,0},{64,32},{96,64},{33,1},{65,33},{97,65},{34,2},{66,34},{98,6... | collective-permute-start | bytes 1572872 | tf_op jit(solution)/shard_map/ppermute | solution.py:84
  25.0 4.6 %collective-permute-start.6 = (f32[8,128,128]{2,1,0:T(8,128)S(1)}, f32[8,128,128]{2,1,0:T(8,128)S(1)}, u32[]{:S(2)}, u32[]{:S(2)}) collective-permute-start(f32[8,128,128]{2,1,0:T(8,128)S(1)} %get-tuple-element.65), channel_id=1, source_target_pairs={{32,0},{64,32},{96,64},{33,1},{65,33},{97,65},{34,2},{66,34},{98,6... | collective-permute-start | bytes 1572872 | tf_op jit(solution)/shard_map/ppermute | solution.py:84
  29.6 3.1 %collective-permute-start.7 = (f32[8,128,128]{2,1,0:T(8,128)S(1)}, f32[8,128,128]{2,1,0:T(8,128)S(1)}, u32[]{:S(2)}, u32[]{:S(2)}) collective-permute-start(f32[8,128,128]{2,1,0:T(8,128)S(1)} %get-tuple-element.66), channel_id=1, source_target_pairs={{4,0},{8,4},{12,8},{16,12},{20,16},{24,20},{28,24},{5,1},{9,5},{13... | collective-permute-start | bytes 1572872 | tf_op jit(solution)/shard_map/ppermute | solution.py:84
  36.5 3.1 %collective-permute-done.5.refs_3_ = f32[8,128,128]{2,1,0:T(8,128)S(1)} collective-permute-done((f32[8,128,128]{2,1,0:T(8,128)S(1)}, f32[8,128,128]{2,1,0:T(8,128)S(1)}, u32[]{:S(2)}, u32[]{:S(2)}) %collective-permute-start.5) | collective-permute-done | bytes 524320 | tf_op jit(solution)/shard_map/ppermute | solution.py:84
  39.7 3.9 %collective-permute-done.6.refs_4_ = f32[8,128,128]{2,1,0:T(8,128)S(1)} collective-permute-done((f32[8,128,128]{2,1,0:T(8,128)S(1)}, f32[8,128,128]{2,1,0:T(8,128)S(1)}, u32[]{:S(2)}, u32[]{:S(2)}) %collective-permute-start.6) | collective-permute-done | bytes 524320 | tf_op jit(solution)/shard_map/ppermute | solution.py:84
  47.6 5.0 %collective-permute-start.9 = (f32[8,128,128]{2,1,0:T(8,128)S(1)}, f32[8,128,128]{2,1,0:T(8,128)S(1)}, u32[]{:S(2)}, u32[]{:S(2)}) collective-permute-start(f32[8,128,128]{2,1,0:T(8,128)S(1)} %get-tuple-element.70), channel_id=1, source_target_pairs={{32,0},{64,32},{96,64},{33,1},{65,33},{97,65},{34,2},{66,34},{98,6... | collective-permute-start | bytes 1572872 | tf_op jit(solution)/shard_map/ppermute | solution.py:84
  54.7 4.5 %collective-permute-start.11 = (f32[8,16,128]{2,1,0:T(8,128)S(1)}, f32[8,16,128]{2,1,0:T(8,128)S(1)}, u32[]{:S(2)}, u32[]{:S(2)}) collective-permute-start(f32[8,16,128]{2,1,0:T(8,128)S(1)} %get-tuple-element.72), channel_id=1, source_target_pairs={{0,1},{1,2},{2,3},{4,5},{5,6},{6,7},{8,9},{9,10},{10,11},{12,13},{... | collective-permute-start | bytes 196616 | tf_op jit(solution)/shard_map/ppermute | solution.py:84
  62.5 3.4 %collective-permute-done.12.refs_7_ = f32[8,16,128]{2,1,0:T(8,128)S(1)} collective-permute-done((f32[8,16,128]{2,1,0:T(8,128)S(1)}, f32[8,16,128]{2,1,0:T(8,128)S(1)}, u32[]{:S(2)}, u32[]{:S(2)}) %collective-permute-start.12) | collective-permute-done | bytes 65568 | tf_op jit(solution)/shard_map/ppermute | solution.py:84
  65.9 3.9 %collective-permute-start.14 = (f32[8,128,128]{2,1,0:T(8,128)S(1)}, f32[8,128,128]{2,1,0:T(8,128)S(1)}, u32[]{:S(2)}, u32[]{:S(2)}) collective-permute-start(f32[8,128,128]{2,1,0:T(8,128)S(1)} %get-tuple-element.77), channel_id=1, source_target_pairs={{32,0},{64,32},{96,64},{33,1},{65,33},{97,65},{34,2},{66,34},{98,6... | collective-permute-start | bytes 1572872 | tf_op jit(solution)/shard_map/ppermute | solution.py:84
  74.1 4.6 %collective-permute-start.17 = (f32[8,128,128]{2,1,0:T(8,128)S(1)}, f32[8,128,128]{2,1,0:T(8,128)S(1)}, u32[]{:S(2)}, u32[]{:S(2)}) collective-permute-start(f32[8,128,128]{2,1,0:T(8,128)S(1)} %get-tuple-element.82), channel_id=1, source_target_pairs={{32,0},{64,32},{96,64},{33,1},{65,33},{97,65},{34,2},{66,34},{98,6... | collective-permute-start | bytes 1572872 | tf_op jit(solution)/shard_map/ppermute | solution.py:84
  86.9 3.6 %collective-permute-start.19 = (f32[8,16,128]{2,1,0:T(8,128)S(1)}, f32[8,16,128]{2,1,0:T(8,128)S(1)}, u32[]{:S(2)}, u32[]{:S(2)}) collective-permute-start(f32[8,16,128]{2,1,0:T(8,128)S(1)} %get-tuple-element.84), channel_id=1, source_target_pairs={{0,1},{1,2},{2,3},{4,5},{5,6},{6,7},{8,9},{9,10},{10,11},{12,13},{... | collective-permute-start | bytes 196616 | tf_op jit(solution)/shard_map/ppermute | solution.py:84
  92.6 2.6 %collective-permute-start.23 = (f32[8,128,128]{2,1,0:T(8,128)S(1)}, f32[8,128,128]{2,1,0:T(8,128)S(1)}, u32[]{:S(2)}, u32[]{:S(2)}) collective-permute-start(f32[8,128,128]{2,1,0:T(8,128)S(1)} %get-tuple-element.90), channel_id=1, source_target_pairs={{4,0},{8,4},{12,8},{16,12},{20,16},{24,20},{28,24},{5,1},{9,5},{13... | collective-permute-start | bytes 1572872 | tf_op jit(solution)/shard_map/ppermute | solution.py:84
  95.2 2.0 %collective-permute-done.20.refs_7_ = f32[8,16,128]{2,1,0:T(8,128)S(1)} collective-permute-done((f32[8,16,128]{2,1,0:T(8,128)S(1)}, f32[8,16,128]{2,1,0:T(8,128)S(1)}, u32[]{:S(2)}, u32[]{:S(2)}) %collective-permute-start.20) | collective-permute-done | bytes 65568 | tf_op jit(solution)/shard_map/ppermute | solution.py:84
  98.5 5.0 %collective-permute-start.22 = (f32[8,128,128]{2,1,0:T(8,128)S(1)}, f32[8,128,128]{2,1,0:T(8,128)S(1)}, u32[]{:S(2)}, u32[]{:S(2)}) collective-permute-start(f32[8,128,128]{2,1,0:T(8,128)S(1)} %get-tuple-element.89), channel_id=1, source_target_pairs={{32,0},{64,32},{96,64},{33,1},{65,33},{97,65},{34,2},{66,34},{98,6... | collective-permute-start | bytes 1572872 | tf_op jit(solution)/shard_map/ppermute | solution.py:84
  107.9 6.5 %collective-permute-done.21.refs_3_ = f32[8,128,128]{2,1,0:T(8,128)S(1)} collective-permute-done((f32[8,128,128]{2,1,0:T(8,128)S(1)}, f32[8,128,128]{2,1,0:T(8,128)S(1)}, u32[]{:S(2)}, u32[]{:S(2)}) %collective-permute-start.21) | collective-permute-done | bytes 524320 | tf_op jit(solution)/shard_map/ppermute | solution.py:84
  117.9 3.5 %collective-permute-start.27 = (f32[8,16,128]{2,1,0:T(8,128)S(1)}, f32[8,16,128]{2,1,0:T(8,128)S(1)}, u32[]{:S(2)}, u32[]{:S(2)}) collective-permute-start(f32[8,16,128]{2,1,0:T(8,128)S(1)} %get-tuple-element.96), channel_id=1, source_target_pairs={{0,1},{1,2},{2,3},{4,5},{5,6},{6,7},{8,9},{9,10},{10,11},{12,13},{... | collective-permute-start | bytes 196616 | tf_op jit(solution)/shard_map/ppermute | solution.py:84
  122.7 4.4 %collective-permute-start.25 = (f32[8,128,128]{2,1,0:T(8,128)S(1)}, f32[8,128,128]{2,1,0:T(8,128)S(1)}, u32[]{:S(2)}, u32[]{:S(2)}) collective-permute-start(f32[8,128,128]{2,1,0:T(8,128)S(1)} %get-tuple-element.94), channel_id=1, source_target_pairs={{32,0},{64,32},{96,64},{33,1},{65,33},{97,65},{34,2},{66,34},{98,6... | collective-permute-start | bytes 1572872 | tf_op jit(solution)/shard_map/ppermute | solution.py:84
  129.1 3.6 %collective-permute-start.31 = (f32[8,128,128]{2,1,0:T(8,128)S(1)}, f32[8,128,128]{2,1,0:T(8,128)S(1)}, u32[]{:S(2)}, u32[]{:S(2)}) collective-permute-start(f32[8,128,128]{2,1,0:T(8,128)S(1)} %get-tuple-element.102), channel_id=1, source_target_pairs={{4,0},{8,4},{12,8},{16,12},{20,16},{24,20},{28,24},{5,1},{9,5},{13... | collective-permute-start | bytes 1572872 | tf_op jit(solution)/shard_map/ppermute | solution.py:84
  134.0 4.6 %collective-permute-start.30 = (f32[8,128,128]{2,1,0:T(8,128)S(1)}, f32[8,128,128]{2,1,0:T(8,128)S(1)}, u32[]{:S(2)}, u32[]{:S(2)}) collective-permute-start(f32[8,128,128]{2,1,0:T(8,128)S(1)} %get-tuple-element.101), channel_id=1, source_target_pairs={{32,0},{64,32},{96,64},{33,1},{65,33},{97,65},{34,2},{66,34},{98,6... | collective-permute-start | bytes 1572872 | tf_op jit(solution)/shard_map/ppermute | solution.py:84
  138.6 2.4 %shard_map.64 = (f32[8,16,144,128]{3,2,1,0:T(8,128)S(1)}, f32[8,16,144,128]{3,2,1,0:T(8,128)S(1)}, f32[8,128,128]{2,1,0:T(8,128)S(1)}) custom-call(f32[8,16,144,128]{3,2,1,0:T(8,128)S(1)} %get-tuple-element.92.refs_0_, f32[8,16,144,128]{3,2,1,0:T(8,128)S(1)} %get-tuple-element.86.refs_0_.refs_1_, ...), custom_call_target="tpu_custom_call", output_to_operand_aliasing={{0}: (0, {}), {1}: (1, {})} | custom-call | flops 12582912 | bytes 12582912 | tf_op jit(solution)/shard_map/pallas_call | solution.py:20
  143.0 4.2 %collective-permute-done.29.refs_3_ = f32[8,128,128]{2,1,0:T(8,128)S(1)} collective-permute-done((f32[8,128,128]{2,1,0:T(8,128)S(1)}, f32[8,128,128]{2,1,0:T(8,128)S(1)}, u32[]{:S(2)}, u32[]{:S(2)}) %collective-permute-start.29) | collective-permute-done | bytes 524320 | tf_op jit(solution)/shard_map/ppermute | solution.py:84
  148.6 2.2 %shard_map.65 = (f32[8,16,144,128]{3,2,1,0:T(8,128)S(1)}, f32[8,128,128]{2,1,0:T(8,128)S(1)}) custom-call(f32[8,16,144,128]{3,2,1,0:T(8,128)S(1)} %get-tuple-element.98.refs_0_, f32[8,16,144,128]{3,2,1,0:T(8,128)S(1)} %get-tuple-element.99.refs_1_, f32[8,16,128,128]{3,2,1,0:T(8,128)S(1)} %get-tuple-element.56.refs_2_, ...), custom_call_target="tpu_custom_call", output_to_operand_aliasing={{0}: (1, {})} | custom-call | flops 12582912 | bytes 12582912 | tf_op jit(solution)/shard_map/pallas_call | solution.py:20
  152.8 5.1 %collective-permute-done.36.q.refs_2_ = f32[8,128,128]{2,1,0:T(8,128)S(1)} collective-permute-done((f32[8,128,128]{2,1,0:T(8,128)S(1)}, f32[8,128,128]{2,1,0:T(8,128)S(1)}, u32[]{:S(2)}, u32[]{:S(2)}) %collective-permute-start.36) | collective-permute-done | bytes 524320 | tf_op jit(solution)/shard_map/ppermute | solution.py:320
  158.0 6.3 %collective-permute-start.37 = (f32[8,128,128]{2,1,0:T(8,128)S(1)}, f32[8,128,128]{2,1,0:T(8,128)S(1)}, u32[]{:S(2)}, u32[]{:S(2)}) collective-permute-start(f32[8,128,128]{2,1,0:T(8,128)S(1)} %shard_map.67), channel_id=1, source_target_pairs={{64,96},{96,64},{65,97},{97,65},{66,98},{98,66},{67,99},{99,67},{6... | collective-permute-start | bytes 1572872 | tf_op jit(solution)/shard_map/ppermute | solution.py:329
  164.3 3.0 %collective-permute-done.33.q.refs_2_ = f32[8,128,128]{2,1,0:T(8,128)S(1)} collective-permute-done((f32[8,128,128]{2,1,0:T(8,128)S(1)}, f32[8,128,128]{2,1,0:T(8,128)S(1)}, u32[]{:S(2)}, u32[]{:S(2)}) %collective-permute-start.33) | collective-permute-done | bytes 524320 | tf_op jit(solution)/shard_map/ppermute | solution.py:320
  167.5 5.9 %collective-permute-start.34 = (f32[8,128,128]{2,1,0:T(8,128)S(1)}, f32[8,128,128]{2,1,0:T(8,128)S(1)}, u32[]{:S(2)}, u32[]{:S(2)}) collective-permute-start(f32[8,128,128]{2,1,0:T(8,128)S(1)} %shard_map.66), channel_id=1, source_target_pairs={{64,96},{96,64},{65,97},{97,65},{66,98},{98,66},{67,99},{99,67},{6... | collective-permute-start | bytes 1572872 | tf_op jit(solution)/shard_map/ppermute | solution.py:329
  173.4 3.4 %shard_map.70 = f32[8,16,128,128]{3,2,1,0:T(8,128)} custom-call(f32[8,16,144,128]{3,2,1,0:T(8,128)S(1)} %get-tuple-element.103.refs_0_.u), custom_call_target="tpu_custom_call" | custom-call | flops 10000000 | bytes 16777216 | tf_op jit(solution)/shard_map/pallas_call | solution.py:20
  176.8 2.1 %shard_map.68.refs_4_ = f32[8,16,128,128]{3,2,1,0:T(8,128)} custom-call(f32[8,16,144,128]{3,2,1,0:T(8,128)S(1)} %get-tuple-element.103.refs_0_.u, f32[8,128,128]{2,1,0:T(8,128)S(1)} %collective-permute-done.35.p.refs_1_, f32[8,128,128]{2,1,0:T(8,128)S(1)} %collective-permute-done.36.q.refs_2_, f32[8,128,128]{2,1,0:T(8,128)S(1)} %collective-permute-done.37.refs_3_), custom_call_target="tpu_custom_call" | custom-call | flops 2097152 | bytes 8388608 | tf_op jit(solution)/shard_map/pallas_call | solution.py:20
  178.9 4.5 %collective-permute-done.34.refs_3_ = f32[8,128,128]{2,1,0:T(8,128)S(1)} collective-permute-done((f32[8,128,128]{2,1,0:T(8,128)S(1)}, f32[8,128,128]{2,1,0:T(8,128)S(1)}, u32[]{:S(2)}, u32[]{:S(2)}) %collective-permute-start.34) | collective-permute-done | bytes 524320 | tf_op jit(solution)/shard_map/ppermute | solution.py:329
  183.4 2.0 %shard_map.69 = f32[8,16,128,128]{3,2,1,0:T(8,128)} custom-call(f32[8,16,144,128]{3,2,1,0:T(8,128)S(1)} %get-tuple-element.103.refs_0_.u, f32[8,128,128]{2,1,0:T(8,128)S(1)} %collective-permute-done.32.p.refs_1_, f32[8,128,128]{2,1,0:T(8,128)S(1)} %collective-permute-done.33.q.refs_2_, ...), custom_call_target="tpu_custom_call", output_to_operand_aliasing={{}: (4, {})} | custom-call | flops 2097152 | bytes 8388608 | tf_op jit(solution)/shard_map/pallas_call | solution.py:20
  (65 shorter events, 54.3 us)
Async XLA Ops:
  2.5 27.1 %collective-permute-start = (f32[8,128,128]{2,1,0:T(8,128)S(1)}, f32[8,128,128]{2,1,0:T(8,128)S(1)}, u32[]{:S(2)}, u32[]{:S(2)}) collective-permute-start(f32[8,128,128]{2,1,0:T(8,128)S(1)} %get-tuple-element.57), channel_id=1, source_target_pairs={{0,32},{32,64},{64,96},{1,33},{33,65},{65,97},{2,34},{34,66},{66,9... | collective-permute-start | bytes 1572872 | tf_op jit(solution)/shard_map/ppermute | solution.py:84
  12.0 11.7 %collective-permute-start.3 = (f32[8,16,128]{2,1,0:T(8,128)S(1)}, f32[8,16,128]{2,1,0:T(8,128)S(1)}, u32[]{:S(2)}, u32[]{:S(2)}) collective-permute-start(f32[8,16,128]{2,1,0:T(8,128)S(1)} %get-tuple-element.60), channel_id=1, source_target_pairs={{0,1},{1,2},{2,3},{4,5},{5,6},{6,7},{8,9},{9,10},{10,11},{12,13},{... | collective-permute-start | bytes 196616 | tf_op jit(solution)/shard_map/ppermute | solution.py:84
  17.1 16.4 %collective-permute-start.1 = (f32[8,128,128]{2,1,0:T(8,128)S(1)}, f32[8,128,128]{2,1,0:T(8,128)S(1)}, u32[]{:S(2)}, u32[]{:S(2)}) collective-permute-start(f32[8,128,128]{2,1,0:T(8,128)S(1)} %get-tuple-element.58), channel_id=1, source_target_pairs={{32,0},{64,32},{96,64},{33,1},{65,33},{97,65},{34,2},{66,34},{98,6... | collective-permute-start | bytes 1572872 | tf_op jit(solution)/shard_map/ppermute | solution.py:84
  21.7 11.8 %collective-permute-start.2 = (f32[8,128,128]{2,1,0:T(8,128)S(1)}, f32[8,128,128]{2,1,0:T(8,128)S(1)}, u32[]{:S(2)}, u32[]{:S(2)}) collective-permute-start(f32[8,128,128]{2,1,0:T(8,128)S(1)} %get-tuple-element.59), channel_id=1, source_target_pairs={{0,4},{4,8},{8,12},{12,16},{16,20},{20,24},{24,28},{1,5},{5,9},{9,... | collective-permute-start | bytes 1572872 | tf_op jit(solution)/shard_map/ppermute | solution.py:84
  23.7 16.0 %collective-permute-start.5 = (f32[8,128,128]{2,1,0:T(8,128)S(1)}, f32[8,128,128]{2,1,0:T(8,128)S(1)}, u32[]{:S(2)}, u32[]{:S(2)}) collective-permute-start(f32[8,128,128]{2,1,0:T(8,128)S(1)} %get-tuple-element.64), channel_id=1, source_target_pairs={{0,32},{32,64},{64,96},{1,33},{33,65},{65,97},{2,34},{34,66},{66,9... | collective-permute-start | bytes 1572872 | tf_op jit(solution)/shard_map/ppermute | solution.py:84
  25.0 18.6 %collective-permute-start.6 = (f32[8,128,128]{2,1,0:T(8,128)S(1)}, f32[8,128,128]{2,1,0:T(8,128)S(1)}, u32[]{:S(2)}, u32[]{:S(2)}) collective-permute-start(f32[8,128,128]{2,1,0:T(8,128)S(1)} %get-tuple-element.65), channel_id=1, source_target_pairs={{32,0},{64,32},{96,64},{33,1},{65,33},{97,65},{34,2},{66,34},{98,6... | collective-permute-start | bytes 1572872 | tf_op jit(solution)/shard_map/ppermute | solution.py:84
  29.6 14.0 %collective-permute-start.7 = (f32[8,128,128]{2,1,0:T(8,128)S(1)}, f32[8,128,128]{2,1,0:T(8,128)S(1)}, u32[]{:S(2)}, u32[]{:S(2)}) collective-permute-start(f32[8,128,128]{2,1,0:T(8,128)S(1)} %get-tuple-element.66), channel_id=1, source_target_pairs={{4,0},{8,4},{12,8},{16,12},{20,16},{24,20},{28,24},{5,1},{9,5},{13... | collective-permute-start | bytes 1572872 | tf_op jit(solution)/shard_map/ppermute | solution.py:84
  44.4 25.4 %collective-permute-start.10 = (f32[8,128,128]{2,1,0:T(8,128)S(1)}, f32[8,128,128]{2,1,0:T(8,128)S(1)}, u32[]{:S(2)}, u32[]{:S(2)}) collective-permute-start(f32[8,128,128]{2,1,0:T(8,128)S(1)} %get-tuple-element.71), channel_id=1, source_target_pairs={{0,4},{4,8},{8,12},{12,16},{16,20},{20,24},{24,28},{1,5},{5,9},{9,... | collective-permute-start | bytes 1572872 | tf_op jit(solution)/shard_map/ppermute | solution.py:84
  46.3 25.4 %collective-permute-start.8 = (f32[8,128,128]{2,1,0:T(8,128)S(1)}, f32[8,128,128]{2,1,0:T(8,128)S(1)}, u32[]{:S(2)}, u32[]{:S(2)}) collective-permute-start(f32[8,128,128]{2,1,0:T(8,128)S(1)} %get-tuple-element.69), channel_id=1, source_target_pairs={{0,32},{32,64},{64,96},{1,33},{33,65},{65,97},{2,34},{34,66},{66,9... | collective-permute-start | bytes 1572872 | tf_op jit(solution)/shard_map/ppermute | solution.py:84
  47.6 24.1 %collective-permute-start.9 = (f32[8,128,128]{2,1,0:T(8,128)S(1)}, f32[8,128,128]{2,1,0:T(8,128)S(1)}, u32[]{:S(2)}, u32[]{:S(2)}) collective-permute-start(f32[8,128,128]{2,1,0:T(8,128)S(1)} %get-tuple-element.70), channel_id=1, source_target_pairs={{32,0},{64,32},{96,64},{33,1},{65,33},{97,65},{34,2},{66,34},{98,6... | collective-permute-start | bytes 1572872 | tf_op jit(solution)/shard_map/ppermute | solution.py:84
  61.2 19.4 %collective-permute-start.13 = (f32[8,128,128]{2,1,0:T(8,128)S(1)}, f32[8,128,128]{2,1,0:T(8,128)S(1)}, u32[]{:S(2)}, u32[]{:S(2)}) collective-permute-start(f32[8,128,128]{2,1,0:T(8,128)S(1)} %get-tuple-element.76), channel_id=1, source_target_pairs={{0,32},{32,64},{64,96},{1,33},{33,65},{65,97},{2,34},{34,66},{66,9... | collective-permute-start | bytes 1572872 | tf_op jit(solution)/shard_map/ppermute | solution.py:84
  65.9 16.2 %collective-permute-start.14 = (f32[8,128,128]{2,1,0:T(8,128)S(1)}, f32[8,128,128]{2,1,0:T(8,128)S(1)}, u32[]{:S(2)}, u32[]{:S(2)}) collective-permute-start(f32[8,128,128]{2,1,0:T(8,128)S(1)} %get-tuple-element.77), channel_id=1, source_target_pairs={{32,0},{64,32},{96,64},{33,1},{65,33},{97,65},{34,2},{66,34},{98,6... | collective-permute-start | bytes 1572872 | tf_op jit(solution)/shard_map/ppermute | solution.py:84
  69.8 12.3 %collective-permute-start.15 = (f32[8,128,128]{2,1,0:T(8,128)S(1)}, f32[8,128,128]{2,1,0:T(8,128)S(1)}, u32[]{:S(2)}, u32[]{:S(2)}) collective-permute-start(f32[8,128,128]{2,1,0:T(8,128)S(1)} %get-tuple-element.78), channel_id=1, source_target_pairs={{4,0},{8,4},{12,8},{16,12},{20,16},{24,20},{28,24},{5,1},{9,5},{13... | collective-permute-start | bytes 1572872 | tf_op jit(solution)/shard_map/ppermute | solution.py:84
  72.8 25.7 %collective-permute-start.16 = (f32[8,128,128]{2,1,0:T(8,128)S(1)}, f32[8,128,128]{2,1,0:T(8,128)S(1)}, u32[]{:S(2)}, u32[]{:S(2)}) collective-permute-start(f32[8,128,128]{2,1,0:T(8,128)S(1)} %get-tuple-element.81), channel_id=1, source_target_pairs={{0,32},{32,64},{64,96},{1,33},{33,65},{65,97},{2,34},{34,66},{66,9... | collective-permute-start | bytes 1572872 | tf_op jit(solution)/shard_map/ppermute | solution.py:84
  74.1 29.5 %collective-permute-start.17 = (f32[8,128,128]{2,1,0:T(8,128)S(1)}, f32[8,128,128]{2,1,0:T(8,128)S(1)}, u32[]{:S(2)}, u32[]{:S(2)}) collective-permute-start(f32[8,128,128]{2,1,0:T(8,128)S(1)} %get-tuple-element.82), channel_id=1, source_target_pairs={{32,0},{64,32},{96,64},{33,1},{65,33},{97,65},{34,2},{66,34},{98,6... | collective-permute-start | bytes 1572872 | tf_op jit(solution)/shard_map/ppermute | solution.py:84
  82.9 20.7 %collective-permute-start.18 = (f32[8,128,128]{2,1,0:T(8,128)S(1)}, f32[8,128,128]{2,1,0:T(8,128)S(1)}, u32[]{:S(2)}, u32[]{:S(2)}) collective-permute-start(f32[8,128,128]{2,1,0:T(8,128)S(1)} %get-tuple-element.83), channel_id=1, source_target_pairs={{0,4},{4,8},{8,12},{12,16},{16,20},{20,24},{24,28},{1,5},{5,9},{9,... | collective-permute-start | bytes 1572872 | tf_op jit(solution)/shard_map/ppermute | solution.py:84
  92.6 15.3 %collective-permute-start.23 = (f32[8,128,128]{2,1,0:T(8,128)S(1)}, f32[8,128,128]{2,1,0:T(8,128)S(1)}, u32[]{:S(2)}, u32[]{:S(2)}) collective-permute-start(f32[8,128,128]{2,1,0:T(8,128)S(1)} %get-tuple-element.90), channel_id=1, source_target_pairs={{4,0},{8,4},{12,8},{16,12},{20,16},{24,20},{28,24},{5,1},{9,5},{13... | collective-permute-start | bytes 1572872 | tf_op jit(solution)/shard_map/ppermute | solution.py:84
  97.2 17.1 %collective-permute-start.21 = (f32[8,128,128]{2,1,0:T(8,128)S(1)}, f32[8,128,128]{2,1,0:T(8,128)S(1)}, u32[]{:S(2)}, u32[]{:S(2)}) collective-permute-start(f32[8,128,128]{2,1,0:T(8,128)S(1)} %get-tuple-element.88), channel_id=1, source_target_pairs={{0,32},{32,64},{64,96},{1,33},{33,65},{65,97},{2,34},{34,66},{66,9... | collective-permute-start | bytes 1572872 | tf_op jit(solution)/shard_map/ppermute | solution.py:84
  98.5 16.5 %collective-permute-start.22 = (f32[8,128,128]{2,1,0:T(8,128)S(1)}, f32[8,128,128]{2,1,0:T(8,128)S(1)}, u32[]{:S(2)}, u32[]{:S(2)}) collective-permute-start(f32[8,128,128]{2,1,0:T(8,128)S(1)} %get-tuple-element.89), channel_id=1, source_target_pairs={{32,0},{64,32},{96,64},{33,1},{65,33},{97,65},{34,2},{66,34},{98,6... | collective-permute-start | bytes 1572872 | tf_op jit(solution)/shard_map/ppermute | solution.py:84
  104.7 29.4 %collective-permute-start.24 = (f32[8,128,128]{2,1,0:T(8,128)S(1)}, f32[8,128,128]{2,1,0:T(8,128)S(1)}, u32[]{:S(2)}, u32[]{:S(2)}) collective-permute-start(f32[8,128,128]{2,1,0:T(8,128)S(1)} %get-tuple-element.93), channel_id=1, source_target_pairs={{0,32},{32,64},{64,96},{1,33},{33,65},{65,97},{2,34},{34,66},{66,9... | collective-permute-start | bytes 1572872 | tf_op jit(solution)/shard_map/ppermute | solution.py:84
  121.4 11.3 %collective-permute-start.28 = (f32[8,16,128]{2,1,0:T(8,128)S(1)}, f32[8,16,128]{2,1,0:T(8,128)S(1)}, u32[]{:S(2)}, u32[]{:S(2)}) collective-permute-start(f32[8,16,128]{2,1,0:T(8,128)S(1)} %get-tuple-element.97), channel_id=1, source_target_pairs={{1,0},{2,1},{3,2},{5,4},{6,5},{7,6},{9,8},{10,9},{11,10},{13,12},{... | collective-permute-start | bytes 196616 | tf_op jit(solution)/shard_map/ppermute | solution.py:84
  122.7 15.9 %collective-permute-start.25 = (f32[8,128,128]{2,1,0:T(8,128)S(1)}, f32[8,128,128]{2,1,0:T(8,128)S(1)}, u32[]{:S(2)}, u32[]{:S(2)}) collective-permute-start(f32[8,128,128]{2,1,0:T(8,128)S(1)} %get-tuple-element.94), channel_id=1, source_target_pairs={{32,0},{64,32},{96,64},{33,1},{65,33},{97,65},{34,2},{66,34},{98,6... | collective-permute-start | bytes 1572872 | tf_op jit(solution)/shard_map/ppermute | solution.py:84
  127.1 11.5 %collective-permute-start.26 = (f32[8,128,128]{2,1,0:T(8,128)S(1)}, f32[8,128,128]{2,1,0:T(8,128)S(1)}, u32[]{:S(2)}, u32[]{:S(2)}) collective-permute-start(f32[8,128,128]{2,1,0:T(8,128)S(1)} %get-tuple-element.95), channel_id=1, source_target_pairs={{0,4},{4,8},{8,12},{12,16},{16,20},{20,24},{24,28},{1,5},{5,9},{9,... | collective-permute-start | bytes 1572872 | tf_op jit(solution)/shard_map/ppermute | solution.py:84
  129.1 13.9 %collective-permute-start.31 = (f32[8,128,128]{2,1,0:T(8,128)S(1)}, f32[8,128,128]{2,1,0:T(8,128)S(1)}, u32[]{:S(2)}, u32[]{:S(2)}) collective-permute-start(f32[8,128,128]{2,1,0:T(8,128)S(1)} %get-tuple-element.102), channel_id=1, source_target_pairs={{4,0},{8,4},{12,8},{16,12},{20,16},{24,20},{28,24},{5,1},{9,5},{13... | collective-permute-start | bytes 1572872 | tf_op jit(solution)/shard_map/ppermute | solution.py:84
  132.7 14.5 %collective-permute-start.29 = (f32[8,128,128]{2,1,0:T(8,128)S(1)}, f32[8,128,128]{2,1,0:T(8,128)S(1)}, u32[]{:S(2)}, u32[]{:S(2)}) collective-permute-start(f32[8,128,128]{2,1,0:T(8,128)S(1)} %get-tuple-element.100), channel_id=1, source_target_pairs={{0,32},{32,64},{64,96},{1,33},{33,65},{65,97},{2,34},{34,66},{66,9... | collective-permute-start | bytes 1572872 | tf_op jit(solution)/shard_map/ppermute | solution.py:84
  134.0 14.6 %collective-permute-start.30 = (f32[8,128,128]{2,1,0:T(8,128)S(1)}, f32[8,128,128]{2,1,0:T(8,128)S(1)}, u32[]{:S(2)}, u32[]{:S(2)}) collective-permute-start(f32[8,128,128]{2,1,0:T(8,128)S(1)} %get-tuple-element.101), channel_id=1, source_target_pairs={{32,0},{64,32},{96,64},{33,1},{65,33},{97,65},{34,2},{66,34},{98,6... | collective-permute-start | bytes 1572872 | tf_op jit(solution)/shard_map/ppermute | solution.py:84
  141.0 16.9 %collective-permute-start.36 = (f32[8,128,128]{2,1,0:T(8,128)S(1)}, f32[8,128,128]{2,1,0:T(8,128)S(1)}, u32[]{:S(2)}, u32[]{:S(2)}) collective-permute-start(f32[8,128,128]{2,1,0:T(8,128)S(1)} %get-tuple-element.105.total), channel_id=1, source_target_pairs={{0,96},{1,97},{2,98},{3,99},{4,100},{5,101},{6,102},{7,103},{8,104... | collective-permute-start | bytes 1572872 | tf_op jit(solution)/shard_map/ppermute | solution.py:320
  142.3 15.6 %collective-permute-start.35 = (f32[8,128,128]{2,1,0:T(8,128)S(1)}, f32[8,128,128]{2,1,0:T(8,128)S(1)}, u32[]{:S(2)}, u32[]{:S(2)}) collective-permute-start(f32[8,128,128]{2,1,0:T(8,128)S(1)} %get-tuple-element.105.total), channel_id=1, source_target_pairs={{0,32},{32,64},{1,33},{33,65},{2,34},{34,66},{3,35},{35,67},{4,36}... | collective-permute-start | bytes 1572872 | tf_op jit(solution)/shard_map/ppermute | solution.py:319
  150.8 16.6 %collective-permute-start.33 = (f32[8,128,128]{2,1,0:T(8,128)S(1)}, f32[8,128,128]{2,1,0:T(8,128)S(1)}, u32[]{:S(2)}, u32[]{:S(2)}) collective-permute-start(f32[8,128,128]{2,1,0:T(8,128)S(1)} %get-tuple-element.104.total), channel_id=1, source_target_pairs={{0,96},{1,97},{2,98},{3,99},{4,100},{5,101},{6,102},{7,103},{8,104... | collective-permute-start | bytes 1572872 | tf_op jit(solution)/shard_map/ppermute | solution.py:320
  152.1 15.3 %collective-permute-start.32 = (f32[8,128,128]{2,1,0:T(8,128)S(1)}, f32[8,128,128]{2,1,0:T(8,128)S(1)}, u32[]{:S(2)}, u32[]{:S(2)}) collective-permute-start(f32[8,128,128]{2,1,0:T(8,128)S(1)} %get-tuple-element.104.total), channel_id=1, source_target_pairs={{0,32},{32,64},{1,33},{33,65},{2,34},{34,66},{3,35},{35,67},{4,36}... | collective-permute-start | bytes 1572872 | tf_op jit(solution)/shard_map/ppermute | solution.py:319
  158.0 18.8 %collective-permute-start.37 = (f32[8,128,128]{2,1,0:T(8,128)S(1)}, f32[8,128,128]{2,1,0:T(8,128)S(1)}, u32[]{:S(2)}, u32[]{:S(2)}) collective-permute-start(f32[8,128,128]{2,1,0:T(8,128)S(1)} %shard_map.67), channel_id=1, source_target_pairs={{64,96},{96,64},{65,97},{97,65},{66,98},{98,66},{67,99},{99,67},{6... | collective-permute-start | bytes 1572872 | tf_op jit(solution)/shard_map/ppermute | solution.py:329
  167.5 15.9 %collective-permute-start.34 = (f32[8,128,128]{2,1,0:T(8,128)S(1)}, f32[8,128,128]{2,1,0:T(8,128)S(1)}, u32[]{:S(2)}, u32[]{:S(2)}) collective-permute-start(f32[8,128,128]{2,1,0:T(8,128)S(1)} %shard_map.66), channel_id=1, source_target_pairs={{64,96},{96,64},{65,97},{97,65},{66,98},{98,66},{67,99},{99,67},{6... | collective-permute-start | bytes 1572872 | tf_op jit(solution)/shard_map/ppermute | solution.py:329
  (6 other events, 45.9 us)
